TPU v7x, 512 devices: a whole 4x8x8 slice. The times are simulated.
512 devices in a mesh: gx: 128 (over z, y, core), gy: 4 (over x).
Axes of the slice: x: 4, y: 8, z: 8, core: 2. Of those that a mesh axis runs over, the one named last changes fastest.
Arguments:
- anomalies: float32 [80, 256, 32, 128], P(None, 'gx', 'gy'), may hold values from -6 to 6
- state_mean: float32 [256, 32, 128], P('gx', 'gy'), may hold values from -6 to 6
- obs_value: float32 [16, 256], P(None, 'gy'), may hold values from -8 to 8
- obs_cell: int32 [16, 256], replicated, may hold values from 0 to 2047
- owner: int32 [16], replicated, may hold values from 0 to 127, as said below
- order: int32 [16], replicated, may hold values from 0 to 15, each once
- root_inv: float32 [16, 256, 256], P(None, 'gy'), as said below
- gain_inv: float32 [16, 256, 256], P(None, 'gy'), as said below
Outputs:
- post_anomalies: float32 [80, 256, 32, 128], P(None, 'gx', 'gy')
- post_mean: float32 [256, 32, 128], P('gx', 'gy')
Inputs may be any that keep to these rules, and one draw needn't show every extreme that they name: `owner`: some batch lies at slab 128 - 2, some at slab 1 and some at slab 128 // 2; the others favour low slabs. `order`: each batch number once. `root_inv`: symmetric. `gain_inv`: symmetric.
All inputs are finite; a program needn't handle non-finite values.
Results may differ from a plain program's by a relative error of at most 0.0001.
Values sent between devices are 32-bit elements; how exact they have to be, the bound alone decides.
A program may use at most 64 MiB of HBM per device.

v0:
```python
import jax
import jax.numpy as jnp
from jax import lax
from jax.sharding import PartitionSpec as P

BATCHES = 16
REACH = 3


def shifted(value, axis, steps):
    count = lax.axis_size(axis)
    pairs = [(source, (source + steps) % count) for source in range(count)]
    return lax.ppermute(value, axis, pairs)


def gather_turned(arrays, axis, dims):
    turned = [jnp.moveaxis(a, dim, 0) for a, dim in zip(arrays, dims)]
    both = jnp.concatenate([t.reshape(len(t), -1) for t in turned], axis=1)
    out, at, done = (lax.all_gather(both, axis, axis=0, tiled=True), 0, [])
    for t, dim in zip(turned, dims):
        slab = out[:, at : at + t[0].size].reshape(-1, *t.shape[1:])
        done.append(jnp.moveaxis(slab, 0, dim))
        at += t[0].size
    return tuple(done)


def product(left_side, right_side):
    return jnp.dot(
        left_side, right_side, precision=lax.Precision.HIGHEST, preferred_element_type=jnp.float32
    )


def prior_relay(masked):
    total = masked
    upward = masked
    downward = masked
    for step in range(REACH):
        upward = shifted(upward, "gx", 1)
        downward = shifted(downward, "gx", -1)
        total = total + upward + downward
    return total


def local(anomalies, state_mean, obs_value, obs_cell, owner, order, root_inv, gain_inv):
    members, lon_dev, lat_dev, levels = anomalies.shape
    cell_count = lon_dev * lat_dev * levels
    quarter = obs_value.shape[1]
    obs_total = obs_cell.shape[1]
    slab_count = lax.axis_size("gx")
    band_count = lax.axis_size("gy")
    column = lax.axis_index("gx")
    band_index = lax.axis_index("gy")
    lon_total = slab_count * lon_dev
    lat_total = band_count * lat_dev
    taper_span = REACH * lon_dev + 1.0
    cell_ids = jnp.arange(cell_count, dtype=jnp.int32)
    cell_lon = column * lon_dev + cell_ids // (lat_dev * levels)
    cell_lat = band_index * lat_dev + cell_ids // levels % lat_dev
    obs_band = jnp.arange(obs_total, dtype=jnp.int32) // quarter

    def assimilate(batch_turn, carried):
        state_rows, mean_row = carried
        batch_id = order[batch_turn]
        root_slab = owner[batch_id]
        is_root = column == root_slab
        cells_of = obs_cell[batch_id]
        local_ids = lax.dynamic_slice_in_dim(cells_of, band_index * quarter, quarter)
        picked = jnp.take(state_rows, local_ids, axis=1)
        innovation = obs_value[batch_id] - jnp.take(mean_row, local_ids)
        root_rows = root_inv[batch_id]
        gain_rows = gain_inv[batch_id]
        joined = jnp.concatenate([picked, innovation[None, :]], axis=0)
        masked = jnp.where(is_root, joined, jnp.zeros_like(joined))
        joined = prior_relay(masked)
        picked, innovation = (joined[:members], joined[members])
        prior_all, innov_all = gather_turned((picked, innovation), "gy", (1, 0))
        weighted = product(prior_all, root_rows.T)
        gain_part = product(gain_rows, innov_all)
        weighted_all, gain_all = gather_turned((weighted, gain_part), "gy", (1, 0))
        obs_lon = root_slab * lon_dev + cells_of // (lat_dev * levels)
        obs_lat = obs_band * lat_dev + cells_of // levels % lat_dev
        slab_gap = jnp.abs(column - root_slab)
        in_reach = jnp.minimum(slab_gap, slab_count - slab_gap) <= REACH

        def near_update(operands):
            rows_now, mean_now = operands
            lon_gap = jnp.abs(obs_lon[:, None] - cell_lon[None, :])
            cycle_gap = jnp.minimum(lon_gap, lon_total - lon_gap)
            lat_gap = jnp.abs(obs_lat[:, None] - cell_lat[None, :])
            taper_rows = jnp.maximum(0.0, 1.0 - cycle_gap.astype(jnp.float32) / taper_span) * (
                1.0 - lat_gap.astype(jnp.float32) / lat_total
            )
            covariance = product(prior_all.T, rows_now) / (members - 1.0)
            gained = taper_rows * covariance
            stacked = jnp.concatenate([weighted_all, gain_all[None, :]], axis=0)
            increment = product(stacked, gained)
            return (rows_now - increment[:members], mean_now + increment[members])

        def keep_all(operands):
            return operands

        return lax.cond(in_reach, near_update, keep_all, (state_rows, mean_row))

    start_rows = anomalies.reshape(members, cell_count)
    start_mean = state_mean.reshape(cell_count)
    final_rows, final_mean = lax.fori_loop(0, BATCHES, assimilate, (start_rows, start_mean))
    return (
        final_rows.reshape(members, lon_dev, lat_dev, levels),
        final_mean.reshape(lon_dev, lat_dev, levels),
    )


def solution(mesh):
    return jax.shard_map(
        local,
        mesh=mesh,
        in_specs=(
            P(None, "gx", "gy", None),
            P("gx", "gy", None),
            P(None, "gy"),
            P(),
            P(),
            P(),
            P(None, "gy", None),
            P(None, "gy", None),
        ),
        out_specs=(P(None, "gx", "gy", None), P("gx", "gy", None)),
        check_vma=False,
    )
```

profile of v0, /device:TPU:1, one launch (start us, length us, event | category | flops | bytes accessed | tf_op | source)
XLA Modules:
  0.0 1038.8 jit_solution(2086697936089289550)
XLA Ops:
  3.4 1034.4 %while.19 = (s32[]{:T(128)}, f32[80,2048]{1,0:T(8,128)S(1)}, f32[2048]{0:T(1024)S(1)}, s32[16]{0:T(128)}, s32[16]{0:T(128)}, /*index=5*/s32[]{:T(128)}, s32[16,2...) while((s32[]{:T(128)}, f32[80,2048]{1,0:T(8,128)S(1)}, ...), condition=%wide.region_3.4_spmd.clone, body=%wide.region_0.3_spmd.clone.sunk | while | flops 1037565760 | bytes 11027220 | solution.py:106
  42.6 9.5 all_gather.26
  54.4 9.1 all_gather.27
  77.1 10.3 collective-permute-start
  106.4 9.1 all_gather.26
  140.5 10.3 collective-permute-start
  169.9 9.1 all_gather.26
  204.0 10.3 collective-permute-start
  233.3 9.1 all_gather.26
  273.0 10.3 collective-permute-start
  302.4 9.1 all_gather.26
  338.9 13.4 %collective-permute-start = (f32[81,64]{0,1:T(8,128)S(1)}, f32[81,64]{0,1:T(8,128)S(1)}, u32[]{:S(2)}, u32[]{:S(2)}) collective-permute-start(f32[81,64]{0,1:T(8,128)S(1)} %maximum_select_fusion.2), channel_id=1, source_target_pairs={{0,508},{4,0},{8,4},{12,8},{16,12},{20,16},{24,20},{28,24},{32,28}... | collective-permute-start | bytes 62216 | tf_op jit(solution)/shard_map/while/body/eval_jaxpr/ppermute | solution.py:13
  405.5 10.3 collective-permute-start
  434.8 9.1 all_gather.26
  474.6 10.3 collective-permute-start
  538.0 10.3 collective-permute-start
  601.5 10.3 collective-permute-start
  665.0 10.3 collective-permute-start
  728.4 10.3 collective-permute-start
  791.9 10.3 collective-permute-start
  855.4 10.3 collective-permute-start
  884.7 9.1 all_gather.26
  918.8 10.3 collective-permute-start
  987.9 10.3 collective-permute-start
  (791 shorter events, 768.1 us)
Async XLA Ops:
  72.0 15.3 %collective-permute-start.3 = (f32[81,64]{0,1:T(8,128)S(1)}, f32[81,64]{0,1:T(8,128)S(1)}, u32[]{:S(2)}, u32[]{:S(2)}) collective-permute-start(f32[81,64]{0,1:T(8,128)S(1)} %maximum_select_fusion.2), channel_id=1, source_target_pairs={{0,4},{4,8},{8,12},{12,16},{16,20},{20,24},{24,28},{28,32},{32,36}... | collective-permute-start | bytes 62216 | tf_op jit(solution)/shard_map/while/body/eval_jaxpr/ppermute | solution.py:13
  135.5 15.4 %collective-permute-start.3 = (f32[81,64]{0,1:T(8,128)S(1)}, f32[81,64]{0,1:T(8,128)S(1)}, u32[]{:S(2)}, u32[]{:S(2)}) collective-permute-start(f32[81,64]{0,1:T(8,128)S(1)} %maximum_select_fusion.2), channel_id=1, source_target_pairs={{0,4},{4,8},{8,12},{12,16},{16,20},{20,24},{24,28},{28,32},{32,36}... | collective-permute-start | bytes 62216 | tf_op jit(solution)/shard_map/while/body/eval_jaxpr/ppermute | solution.py:13
  140.5 12.2 %collective-permute-start = (f32[81,64]{0,1:T(8,128)S(1)}, f32[81,64]{0,1:T(8,128)S(1)}, u32[]{:S(2)}, u32[]{:S(2)}) collective-permute-start(f32[81,64]{0,1:T(8,128)S(1)} %maximum_select_fusion.2), channel_id=1, source_target_pairs={{0,508},{4,0},{8,4},{12,8},{16,12},{20,16},{24,20},{28,24},{32,28}... | collective-permute-start | bytes 62216 | tf_op jit(solution)/shard_map/while/body/eval_jaxpr/ppermute | solution.py:13
  199.0 15.4 %collective-permute-start.3 = (f32[81,64]{0,1:T(8,128)S(1)}, f32[81,64]{0,1:T(8,128)S(1)}, u32[]{:S(2)}, u32[]{:S(2)}) collective-permute-start(f32[81,64]{0,1:T(8,128)S(1)} %maximum_select_fusion.2), channel_id=1, source_target_pairs={{0,4},{4,8},{8,12},{12,16},{16,20},{20,24},{24,28},{28,32},{32,36}... | collective-permute-start | bytes 62216 | tf_op jit(solution)/shard_map/while/body/eval_jaxpr/ppermute | solution.py:13
  204.0 12.2 %collective-permute-start = (f32[81,64]{0,1:T(8,128)S(1)}, f32[81,64]{0,1:T(8,128)S(1)}, u32[]{:S(2)}, u32[]{:S(2)}) collective-permute-start(f32[81,64]{0,1:T(8,128)S(1)} %maximum_select_fusion.2), channel_id=1, source_target_pairs={{0,508},{4,0},{8,4},{12,8},{16,12},{20,16},{24,20},{28,24},{32,28}... | collective-permute-start | bytes 62216 | tf_op jit(solution)/shard_map/while/body/eval_jaxpr/ppermute | solution.py:13
  268.0 15.4 %collective-permute-start.3 = (f32[81,64]{0,1:T(8,128)S(1)}, f32[81,64]{0,1:T(8,128)S(1)}, u32[]{:S(2)}, u32[]{:S(2)}) collective-permute-start(f32[81,64]{0,1:T(8,128)S(1)} %maximum_select_fusion.2), channel_id=1, source_target_pairs={{0,4},{4,8},{8,12},{12,16},{16,20},{20,24},{24,28},{28,32},{32,36}... | collective-permute-start | bytes 62216 | tf_op jit(solution)/shard_map/while/body/eval_jaxpr/ppermute | solution.py:13
  273.0 12.2 %collective-permute-start = (f32[81,64]{0,1:T(8,128)S(1)}, f32[81,64]{0,1:T(8,128)S(1)}, u32[]{:S(2)}, u32[]{:S(2)}) collective-permute-start(f32[81,64]{0,1:T(8,128)S(1)} %maximum_select_fusion.2), channel_id=1, source_target_pairs={{0,508},{4,0},{8,4},{12,8},{16,12},{20,16},{24,20},{28,24},{32,28}... | collective-permute-start | bytes 62216 | tf_op jit(solution)/shard_map/while/body/eval_jaxpr/ppermute | solution.py:13
  337.0 15.4 %collective-permute-start.3 = (f32[81,64]{0,1:T(8,128)S(1)}, f32[81,64]{0,1:T(8,128)S(1)}, u32[]{:S(2)}, u32[]{:S(2)}) collective-permute-start(f32[81,64]{0,1:T(8,128)S(1)} %maximum_select_fusion.2), channel_id=1, source_target_pairs={{0,4},{4,8},{8,12},{12,16},{16,20},{20,24},{24,28},{28,32},{32,36}... | collective-permute-start | bytes 62216 | tf_op jit(solution)/shard_map/while/body/eval_jaxpr/ppermute | solution.py:13
  338.9 15.4 %collective-permute-start = (f32[81,64]{0,1:T(8,128)S(1)}, f32[81,64]{0,1:T(8,128)S(1)}, u32[]{:S(2)}, u32[]{:S(2)}) collective-permute-start(f32[81,64]{0,1:T(8,128)S(1)} %maximum_select_fusion.2), channel_id=1, source_target_pairs={{0,508},{4,0},{8,4},{12,8},{16,12},{20,16},{24,20},{28,24},{32,28}... | collective-permute-start | bytes 62216 | tf_op jit(solution)/shard_map/while/body/eval_jaxpr/ppermute | solution.py:13
  400.5 15.4 %collective-permute-start.3 = (f32[81,64]{0,1:T(8,128)S(1)}, f32[81,64]{0,1:T(8,128)S(1)}, u32[]{:S(2)}, u32[]{:S(2)}) collective-permute-start(f32[81,64]{0,1:T(8,128)S(1)} %maximum_select_fusion.2), channel_id=1, source_target_pairs={{0,4},{4,8},{8,12},{12,16},{16,20},{20,24},{24,28},{28,32},{32,36}... | collective-permute-start | bytes 62216 | tf_op jit(solution)/shard_map/while/body/eval_jaxpr/ppermute | solution.py:13
  469.5 15.4 %collective-permute-start.3 = (f32[81,64]{0,1:T(8,128)S(1)}, f32[81,64]{0,1:T(8,128)S(1)}, u32[]{:S(2)}, u32[]{:S(2)}) collective-permute-start(f32[81,64]{0,1:T(8,128)S(1)} %maximum_select_fusion.2), channel_id=1, source_target_pairs={{0,4},{4,8},{8,12},{12,16},{16,20},{20,24},{24,28},{28,32},{32,36}... | collective-permute-start | bytes 62216 | tf_op jit(solution)/shard_map/while/body/eval_jaxpr/ppermute | solution.py:13
  533.0 15.4 %collective-permute-start.3 = (f32[81,64]{0,1:T(8,128)S(1)}, f32[81,64]{0,1:T(8,128)S(1)}, u32[]{:S(2)}, u32[]{:S(2)}) collective-permute-start(f32[81,64]{0,1:T(8,128)S(1)} %maximum_select_fusion.2), channel_id=1, source_target_pairs={{0,4},{4,8},{8,12},{12,16},{16,20},{20,24},{24,28},{28,32},{32,36}... | collective-permute-start | bytes 62216 | tf_op jit(solution)/shard_map/while/body/eval_jaxpr/ppermute | solution.py:13
  538.0 12.2 %collective-permute-start = (f32[81,64]{0,1:T(8,128)S(1)}, f32[81,64]{0,1:T(8,128)S(1)}, u32[]{:S(2)}, u32[]{:S(2)}) collective-permute-start(f32[81,64]{0,1:T(8,128)S(1)} %maximum_select_fusion.2), channel_id=1, source_target_pairs={{0,508},{4,0},{8,4},{12,8},{16,12},{20,16},{24,20},{28,24},{32,28}... | collective-permute-start | bytes 62216 | tf_op jit(solution)/shard_map/while/body/eval_jaxpr/ppermute | solution.py:13
  596.4 15.4 %collective-permute-start.3 = (f32[81,64]{0,1:T(8,128)S(1)}, f32[81,64]{0,1:T(8,128)S(1)}, u32[]{:S(2)}, u32[]{:S(2)}) collective-permute-start(f32[81,64]{0,1:T(8,128)S(1)} %maximum_select_fusion.2), channel_id=1, source_target_pairs={{0,4},{4,8},{8,12},{12,16},{16,20},{20,24},{24,28},{28,32},{32,36}... | collective-permute-start | bytes 62216 | tf_op jit(solution)/shard_map/while/body/eval_jaxpr/ppermute | solution.py:13
  601.5 12.2 %collective-permute-start = (f32[81,64]{0,1:T(8,128)S(1)}, f32[81,64]{0,1:T(8,128)S(1)}, u32[]{:S(2)}, u32[]{:S(2)}) collective-permute-start(f32[81,64]{0,1:T(8,128)S(1)} %maximum_select_fusion.2), channel_id=1, source_target_pairs={{0,508},{4,0},{8,4},{12,8},{16,12},{20,16},{24,20},{28,24},{32,28}... | collective-permute-start | bytes 62216 | tf_op jit(solution)/shard_map/while/body/eval_jaxpr/ppermute | solution.py:13
  659.9 15.4 %collective-permute-start.3 = (f32[81,64]{0,1:T(8,128)S(1)}, f32[81,64]{0,1:T(8,128)S(1)}, u32[]{:S(2)}, u32[]{:S(2)}) collective-permute-start(f32[81,64]{0,1:T(8,128)S(1)} %maximum_select_fusion.2), channel_id=1, source_target_pairs={{0,4},{4,8},{8,12},{12,16},{16,20},{20,24},{24,28},{28,32},{32,36}... | collective-permute-start | bytes 62216 | tf_op jit(solution)/shard_map/while/body/eval_jaxpr/ppermute | solution.py:13
  723.4 15.4 %collective-permute-start.3 = (f32[81,64]{0,1:T(8,128)S(1)}, f32[81,64]{0,1:T(8,128)S(1)}, u32[]{:S(2)}, u32[]{:S(2)}) collective-permute-start(f32[81,64]{0,1:T(8,128)S(1)} %maximum_select_fusion.2), channel_id=1, source_target_pairs={{0,4},{4,8},{8,12},{12,16},{16,20},{20,24},{24,28},{28,32},{32,36}... | collective-permute-start | bytes 62216 | tf_op jit(solution)/shard_map/while/body/eval_jaxpr/ppermute | solution.py:13
  786.8 15.4 %collective-permute-start.3 = (f32[81,64]{0,1:T(8,128)S(1)}, f32[81,64]{0,1:T(8,128)S(1)}, u32[]{:S(2)}, u32[]{:S(2)}) collective-permute-start(f32[81,64]{0,1:T(8,128)S(1)} %maximum_select_fusion.2), channel_id=1, source_target_pairs={{0,4},{4,8},{8,12},{12,16},{16,20},{20,24},{24,28},{28,32},{32,36}... | collective-permute-start | bytes 62216 | tf_op jit(solution)/shard_map/while/body/eval_jaxpr/ppermute | solution.py:13
  791.9 12.2 %collective-permute-start = (f32[81,64]{0,1:T(8,128)S(1)}, f32[81,64]{0,1:T(8,128)S(1)}, u32[]{:S(2)}, u32[]{:S(2)}) collective-permute-start(f32[81,64]{0,1:T(8,128)S(1)} %maximum_select_fusion.2), channel_id=1, source_target_pairs={{0,508},{4,0},{8,4},{12,8},{16,12},{20,16},{24,20},{28,24},{32,28}... | collective-permute-start | bytes 62216 | tf_op jit(solution)/shard_map/while/body/eval_jaxpr/ppermute | solution.py:13
  850.3 15.4 %collective-permute-start.3 = (f32[81,64]{0,1:T(8,128)S(1)}, f32[81,64]{0,1:T(8,128)S(1)}, u32[]{:S(2)}, u32[]{:S(2)}) collective-permute-start(f32[81,64]{0,1:T(8,128)S(1)} %maximum_select_fusion.2), channel_id=1, source_target_pairs={{0,4},{4,8},{8,12},{12,16},{16,20},{20,24},{24,28},{28,32},{32,36}... | collective-permute-start | bytes 62216 | tf_op jit(solution)/shard_map/while/body/eval_jaxpr/ppermute | solution.py:13
  855.4 12.2 %collective-permute-start = (f32[81,64]{0,1:T(8,128)S(1)}, f32[81,64]{0,1:T(8,128)S(1)}, u32[]{:S(2)}, u32[]{:S(2)}) collective-permute-start(f32[81,64]{0,1:T(8,128)S(1)} %maximum_select_fusion.2), channel_id=1, source_target_pairs={{0,508},{4,0},{8,4},{12,8},{16,12},{20,16},{24,20},{28,24},{32,28}... | collective-permute-start | bytes 62216 | tf_op jit(solution)/shard_map/while/body/eval_jaxpr/ppermute | solution.py:13
  913.8 15.4 %collective-permute-start.3 = (f32[81,64]{0,1:T(8,128)S(1)}, f32[81,64]{0,1:T(8,128)S(1)}, u32[]{:S(2)}, u32[]{:S(2)}) collective-permute-start(f32[81,64]{0,1:T(8,128)S(1)} %maximum_select_fusion.2), channel_id=1, source_target_pairs={{0,4},{4,8},{8,12},{12,16},{16,20},{20,24},{24,28},{28,32},{32,36}... | collective-permute-start | bytes 62216 | tf_op jit(solution)/shard_map/while/body/eval_jaxpr/ppermute | solution.py:13
  918.8 12.2 %collective-permute-start = (f32[81,64]{0,1:T(8,128)S(1)}, f32[81,64]{0,1:T(8,128)S(1)}, u32[]{:S(2)}, u32[]{:S(2)}) collective-permute-start(f32[81,64]{0,1:T(8,128)S(1)} %maximum_select_fusion.2), channel_id=1, source_target_pairs={{0,508},{4,0},{8,4},{12,8},{16,12},{20,16},{24,20},{28,24},{32,28}... | collective-permute-start | bytes 62216 | tf_op jit(solution)/shard_map/while/body/eval_jaxpr/ppermute | solution.py:13
  982.8 15.4 %collective-permute-start.3 = (f32[81,64]{0,1:T(8,128)S(1)}, f32[81,64]{0,1:T(8,128)S(1)}, u32[]{:S(2)}, u32[]{:S(2)}) collective-permute-start(f32[81,64]{0,1:T(8,128)S(1)} %maximum_select_fusion.2), channel_id=1, source_target_pairs={{0,4},{4,8},{8,12},{12,16},{16,20},{20,24},{24,28},{28,32},{32,36}... | collective-permute-start | bytes 62216 | tf_op jit(solution)/shard_map/while/body/eval_jaxpr/ppermute | solution.py:13
  (73 other events, 663.2 us)
where the time goes:
time: 1050 us; the launch traced here: 1040 us
  starting transfers between devices  526 us (50%)
  blocking collectives  292 us (28%)
  local copies, waits for them, and re-layouts  98.2 us (9%)
  loops' own time  62 us (6%)
  matrix products  51.1 us (5%)
    ppermute x96, starting transfers between devices, shifted(): return lax.ppermute(value, axis, pairs)  526 us
    all_gather x32, blocking collectives, gather_turned(): out, at, done = (lax.all_gather(both, axis, axis=0, tiled=True), 0, [])  292 us
    another operation x1, loops' own time, local(): lax.fori_loop(0, BATCHES, assimilate, (start_rows, start_mean))  58.9 us
    dot_general x40, matrix products, product(): jnp.dot(left_side, right_side, precision=lax.Precision.HIGHEST, preferred...  51.1 us
  transfers between devices with their start and end apart: 96, of which 0 were waited for; matrix products, arithmetic and copies ran while one was open for 0% of the time, Pallas kernels for 0%

commit v1 on v0

v1 whole, which is shorter than its diff:
```python
import functools

import jax
import jax.numpy as jnp
from jax import lax
from jax.experimental import pallas as pl
from jax.experimental.pallas import tpu as pltpu
from jax.sharding import PartitionSpec as P

MEMBERS = 80
OBS = 256
BATCHES = 16
REACH = 3
SLABS = 128
BANDS = 4
NLON = 256
NLAT = 32
QUARTER = 64
CELLS = 2048
GROUPS = 16
ROWS = 96
HALF = 48
PAIRS = 8
RING = 8
MESH = pl.DeviceIdType.MESH
F32 = jnp.float32
BF16 = jnp.bfloat16


def dist(a, b):
    gap = jnp.abs(a - b)
    return jnp.minimum(gap, SLABS - gap)


def split(value):
    high = value.astype(BF16)
    return high, (value - high.astype(F32)).astype(BF16)


def dot(left, right):
    return jnp.dot(left, right, preferred_element_type=F32)


def dot3(left_high, left_low, right_high, right_low):
    return dot(left_high, right_high) + (dot(left_high, right_low) + dot(left_low, right_high))


def load_state(anom_ref, mean_ref, state):
    tail = lax.broadcasted_iota(jnp.int32, (16, 128), 0)
    for c in range(GROUPS):
        lanes = pl.ds(c * 128, 128)
        state[0:MEMBERS, lanes] = anom_ref[pl.ds(c, MEMBERS, stride=GROUPS), :]
        state[MEMBERS:ROWS, lanes] = jnp.where(tail == 0, -mean_ref[pl.ds(c, 1), :], 0.0)


def prep_kernel(
    order_s, owner_s, anom_ref, mean_ref, cell_ref, value_ref, root_ref, gain_ref,
    packet_ref, rows_ref, table_s,
    state, held, need_s, in_sem, out_sem,
):
    column = lax.axis_index("gx")
    band = lax.axis_index("gy")
    chip_low = column - lax.rem(column, 2)

    for t in reversed(range(BATCHES)):
        slab = owner_s[order_s[t]]
        near = jnp.minimum(dist(slab, chip_low), dist(slab, chip_low + 1)) <= REACH
        need = jnp.where(near, 1, 0)

        def later(s, need, slab=slab):
            linked = dist(owner_s[order_s[s]], slab) <= REACH
            return jnp.where(linked, need | need_s[s], need)

        need_s[t] = lax.fori_loop(t + 1, BATCHES, later, need)

    def listing(t, count):
        @pl.when(need_s[t] == 1)
        def _():
            table_s[1 + count] = order_s[t]

        return count + need_s[t]

    count = lax.fori_loop(0, BATCHES, listing, 0)
    table_s[0] = count

    def fetch(i, which, source):
        return pltpu.make_async_copy(source, held.at[i, which], in_sem.at[i, which])

    def start_fetch(i, carry):
        batch = table_s[1 + i]
        fetch(i, 0, root_ref.at[batch]).start()
        fetch(i, 1, gain_ref.at[batch]).start()
        return carry

    lax.fori_loop(0, count, start_fetch, 0)

    lane = lax.broadcasted_iota(jnp.int32, (8, 128), 1)
    low = 2 * lax.rem(lane, SLABS // 2)
    slabs = [owner_s[order_s[t]] for t in range(BATCHES)]
    needs = [None] * BATCHES
    total = jnp.zeros((8, 128), jnp.int32)
    for t in reversed(range(BATCHES)):
        near = jnp.minimum(dist(slabs[t], low), dist(slabs[t], low + 1)) <= REACH
        need = jnp.where(near, 1, 0)
        for s in range(t + 1, BATCHES):
            linked = jnp.where(dist(slabs[s], slabs[t]) <= REACH, 1, 0)
            need = need | (needs[s] * linked)
        needs[t] = need
        total = total + need
    table_s[BATCHES + 1] = jnp.max(total)

    packet_ref[...] = jnp.zeros_like(packet_ref)
    load_state(anom_ref, mean_ref, state)

    def pick(batch, carry):
        @pl.when(owner_s[batch] == column)
        def _():
            half = batch // PAIRS
            pair = lax.rem(batch, PAIRS)
            cells = jnp.broadcast_to(cell_ref[pl.ds(batch, 1), :], (8, OBS))
            shift = lax.rem(half * QUARTER - band * QUARTER + OBS, OBS)
            mine = pltpu.roll(cells, shift, 1)[0:1, 0:128]
            spot = lax.broadcasted_iota(jnp.int32, (1, 128), 1)
            valid = (spot // QUARTER) == half
            mine = jnp.where(valid, mine, -1)
            picked = jnp.zeros((ROWS, 128), F32)
            step = 512
            for at in range(0, CELLS, step):
                ids = lax.broadcasted_iota(jnp.int32, (step, 128), 0) + at
                hot = jnp.where(ids == mine, 1.0, 0.0).astype(BF16)
                block = state[:, pl.ds(at, step)]
                high = block.astype(BF16)
                rest = block - high.astype(F32)
                mid = rest.astype(BF16)
                last = (rest - mid.astype(F32)).astype(BF16)
                picked = picked + (dot(high, hot) + (dot(mid, hot) + dot(last, hot)))
            row = lax.broadcasted_iota(jnp.int32, (ROWS, 128), 0)
            seen = jnp.where(valid, value_ref[pl.ds(batch, 1), :], 0.0)
            picked = picked + jnp.where(row == MEMBERS, seen, 0.0)
            packet_ref[pair] = packet_ref[pair] + picked

        return carry

    lax.fori_loop(0, BATCHES, pick, 0)

    def put(i):
        return pltpu.make_async_copy(held.at[i], rows_ref.at[i], out_sem.at[i])

    def pass_on(i, carry):
        fetch(i, 0, root_ref.at[0]).wait()
        fetch(i, 1, gain_ref.at[0]).wait()
        put(i).start()
        return carry

    def finish(i, carry):
        put(i).wait()
        return carry

    lax.fori_loop(0, count, pass_on, 0)
    lax.fori_loop(0, count, finish, 0)


def comm_kernel(
    listed, packet_ref, rows_ref, spread_ref, full_ref,
    mixed, rx_core, rx_y, plane, rx_z,
    core_s, core_r, y_s, y_r, z_s, z_r, back_s, back_r, x_s, x_r, pair_s, pair_r,
    mat_s, mat_r, twin_s, twin_r,
):
    column = lax.axis_index("gx")
    band = lax.axis_index("gy")
    core = lax.rem(column, 2)
    y = lax.rem(column // 2, RING)
    z = column // (2 * RING)
    partner = (z * RING + y) * 2 + 1 - core

    def at_y(step):
        return (z * RING + lax.rem(y + step, RING)) * 2 + core

    def at_z(step):
        return (lax.rem(z + step, RING) * RING + y) * 2 + core

    def at_x(step):
        return lax.rem(band + step, BANDS)

    def copy(src, dst, send, recv, gx, gy):
        return pltpu.make_async_remote_copy(
            src_ref=src, dst_ref=dst, send_sem=send, recv_sem=recv,
            device_id=(gx, gy), device_id_type=MESH,
        )

    barrier = pltpu.get_barrier_semaphore()
    peers = [(partner, band)]
    peers += [(at_y(d), band) for d in range(1, RING)]
    peers += [(at_z(d), band) for d in range(1, RING)]
    peers += [(column, at_x(d)) for d in range(1, BANDS)]
    for peer in peers:
        pl.semaphore_signal(barrier, inc=1, device_id=peer, device_id_type=MESH)
    pl.semaphore_wait(barrier, len(peers))

    mine = pl.ds(pl.multiple_of(core * HALF, 8), HALF)
    other = pl.ds(pl.multiple_of((1 - core) * HALF, 8), HALF)
    sends = []

    def go(descriptor):
        descriptor.start()
        sends.append(descriptor)

    swap = copy(packet_ref.at[:, other, :], rx_core, core_s, core_r, partner, band)
    go(swap)

    def my_rows(of):
        return pl.ds(pl.multiple_of(of * QUARTER, 8), QUARTER)

    source = rows_ref.at[pl.ds(0, listed), core]
    for d in range(1, BANDS):
        go(copy(source, full_ref.at[:, core, my_rows(band), :], mat_s.at[d - 1], mat_r.at[d - 1], column, at_x(d)))

    swap.wait_recv()
    mixed[...] = packet_ref[:, mine, :] + rx_core[...]

    for d in (4, 3, 5, 2, 6, 1, 7):
        go(copy(mixed.at[lax.rem(y + d, RING)], rx_y.at[d - 1], y_s.at[d - 1], y_r.at[d - 1], at_y(d), band))
    part = mixed[y]
    for d in (1, 7, 2, 6, 3, 5, 4):
        copy(mixed.at[0], rx_y.at[d - 1], y_s.at[d - 1], y_r.at[d - 1], at_y(RING - d), band).wait_recv()
        part = part + rx_y[d - 1]
    plane[...] = part

    for d in (4, 3, 5, 2, 6, 1, 7):
        go(copy(plane, rx_z.at[d - 1], z_s.at[d - 1], z_r.at[d - 1], at_z(d), band))
    for d in (1, 7, 2, 6, 3, 5, 4):
        copy(plane, rx_z.at[d - 1], z_s.at[d - 1], z_r.at[d - 1], at_z(RING - d), band).wait_recv()
        part = part + rx_z[d - 1]
    spread_ref[band, y, mine, :] = part

    def slot(x, home):
        return spread_ref.at[x, home, mine, :]

    own = slot(band, y)
    for d in (4, 3, 5, 2, 6, 1, 7):
        go(copy(own, own, back_s.at[d - 1], back_r.at[d - 1], at_y(d), band))

    homes = [(0, y)] + [(d, lax.rem(y + RING - d, RING)) for d in (1, 7, 2, 6, 3, 5, 4)]
    for d, home in homes:
        here = slot(band, home)
        if d:
            copy(here, here, back_s.at[d - 1], back_r.at[d - 1], at_y(RING - d), band).wait_recv()
        for e in (2, 1, 3):
            go(copy(here, here, x_s.at[e - 1, d], x_r.at[e - 1, d], column, at_x(e)))
        go(copy(here, here, pair_s.at[0, d], pair_r.at[0, d], partner, band))
    for d, home in homes:
        for e in (1, 3, 2):
            here = slot(at_x(BANDS - e), home)
            copy(here, here, x_s.at[e - 1, d], x_r.at[e - 1, d], column, at_x(BANDS - e)).wait_recv()
            go(copy(here, here, pair_s.at[e, d], pair_r.at[e, d], partner, band))

    for d in (1, 3, 2):
        came = full_ref.at[:, core, my_rows(at_x(BANDS - d)), :]
        copy(came, came, mat_s.at[d - 1], mat_r.at[d - 1], column, at_x(BANDS - d)).wait_recv()
        go(copy(came, came, twin_s.at[d - 1], twin_r.at[d - 1], partner, band))

    for d, home in homes:
        for e in range(BANDS):
            there = spread_ref.at[at_x(BANDS - e), home, other, :]
            copy(there, there, pair_s.at[e, d], pair_r.at[e, d], partner, band).wait_recv()
    for d in (1, 3, 2):
        came = full_ref.at[:, 1 - core, my_rows(at_x(BANDS - d)), :]
        copy(came, came, twin_s.at[d - 1], twin_r.at[d - 1], partner, band).wait_recv()
    for descriptor in sends:
        descriptor.wait_send()


def solve_kernel(
    owner_s, table_s, anom_ref, mean_ref, cell_ref, spread_ref, rows_ref, full_ref,
    out_anom_ref, out_mean_ref,
    state, prior, mats, left_high, left_low, middle, mat_sem,
):
    column = lax.axis_index("gx")
    band = lax.axis_index("gy")
    count = table_s[0]

    def fetch(i, x, from_own):
        rows = pl.ds(x * QUARTER, QUARTER)
        source = rows_ref.at[i] if from_own else full_ref.at[i, :, rows, :]
        return pltpu.make_async_copy(source, mats.at[i, :, rows, :], mat_sem.at[i, x])

    def start(i, carry):
        for x in range(BANDS):
            @pl.when(band == x)
            def _():
                fetch(i, x, True).start()

            @pl.when(band != x)
            def _():
                fetch(i, x, False).start()

        return carry

    lax.fori_loop(0, count, start, 0)
    load_state(anom_ref, mean_ref, state)

    lane = lax.broadcasted_iota(jnp.int32, (ROWS, 128), 1)

    def assemble(i, carry):
        batch = table_s[1 + i]
        half = batch // PAIRS
        pair = lax.rem(batch, PAIRS)
        for x in (0, 2):
            first = pltpu.roll(spread_ref[x, pair], half * QUARTER, 1)
            second = pltpu.roll(spread_ref[x + 1, pair], (1 - half) * QUARTER, 1)
            prior[i, :, pl.ds(x * QUARTER, 128)] = jnp.where(lane < QUARTER, first, second)
        return carry

    lax.fori_loop(0, count, assemble, 0)

    spot = lax.broadcasted_iota(jnp.int32, (1, OBS), 1)
    scale = 1.0 / (7.0 * 32.0 * 79.0)

    def places(batch):
        cells = cell_ref[pl.ds(batch, 1), :]
        lon = owner_s[batch] * 2 + cells // 1024
        lat = (spot // QUARTER) * 8 + lax.rem(cells // 128, 8)
        return lon, lat

    def taper(lon_gap, lat_gap):
        lon_gap = jnp.minimum(lon_gap, NLON - lon_gap)
        return (
            jnp.maximum(7 - lon_gap, 0).astype(F32) * (NLAT - lat_gap).astype(F32) * scale
        )

    row = lax.broadcasted_iota(jnp.int32, (ROWS, OBS), 0)

    def assimilate(i, carry):
        batch = table_s[1 + i]
        slab = owner_s[batch]
        for x in range(BANDS):
            fetch(i, x, False).wait()
        z = prior[i]
        z_high, z_low = split(z)
        root_high, root_low = split(mats[i, 0])
        gain_high, gain_low = split(mats[i, 1])
        weighted = dot3(z_high, z_low, root_high, root_low)
        gained = dot3(z_high[MEMBERS:ROWS], z_low[MEMBERS:ROWS], gain_high, gain_low)
        weights = jnp.concatenate([weighted[0:MEMBERS], gained], axis=0)
        turned = jnp.transpose(jnp.where(row < MEMBERS, z, 0.0))
        turned_high, turned_low = split(turned)
        lon, lat = places(batch)
        both = jnp.concatenate(
            [jnp.broadcast_to(lon, (8, OBS)), jnp.broadcast_to(lat, (8, OBS))], axis=0
        ).astype(F32)
        upright = jnp.transpose(both).astype(jnp.int32)
        lon_col = upright[:, 0:1]
        lat_col = upright[:, 8:9]

        weights_high, weights_low = split(weights)

        def later(j, carry):
            other = table_s[1 + j]

            @pl.when(dist(owner_s[other], slab) <= REACH)
            def _():
                held = prior[j]
                held_high, held_low = split(held)
                covariance = dot3(turned_high, turned_low, held_high, held_low)
                lon_j, lat_j = places(other)
                gain = covariance * taper(jnp.abs(lon_col - lon_j), jnp.abs(lat_col - lat_j))
                gain_h, gain_l = split(gain)
                prior[j] = held - dot3(weights_high, weights_low, gain_h, gain_l)

            return carry

        lax.fori_loop(i + 1, count, later, 0)

        @pl.when(dist(slab, column) <= REACH)
        def _():
            for c in range(GROUPS):
                cell_lon = column * 2 + c // 8
                cell_lat = band * 8 + c % 8
                factor = taper(jnp.abs(lon - cell_lon), jnp.abs(lat - cell_lat))
                high, low = split(weights * factor)
                left_high[pl.ds(c * ROWS, ROWS), :] = high
                left_low[pl.ds(c * ROWS, ROWS), :] = low
            middle[...] = dot3(left_high[...], left_low[...], turned_high, turned_low)
            for c in range(GROUPS):
                lanes = pl.ds(c * 128, 128)
                block = state[:, lanes]
                m_high, m_low = split(middle[pl.ds(c * ROWS, ROWS), :])
                b_high, b_low = split(block)
                state[:, lanes] = block - dot3(m_high, m_low, b_high, b_low)

        return carry

    lax.fori_loop(0, count, assimilate, 0)

    for c in range(GROUPS):
        lanes = pl.ds(c * 128, 128)
        out_anom_ref[pl.ds(c, MEMBERS, stride=GROUPS), :] = state[0:MEMBERS, lanes]
        out_mean_ref[pl.ds(c, 1), :] = -state[pl.ds(MEMBERS, 1), lanes]


VMEM = pl.BlockSpec(memory_space=pltpu.VMEM)
SMEM = pl.BlockSpec(memory_space=pltpu.SMEM)
HBM = pl.BlockSpec(memory_space=pl.ANY)
DMA = pltpu.SemaphoreType.DMA


def exchange(listed, collective_id, packet, rows):
    return pl.pallas_call(
        functools.partial(comm_kernel, listed),
        name="exchange",
        out_shape=(
            jax.ShapeDtypeStruct((BANDS, PAIRS, ROWS, 128), F32),
            jax.ShapeDtypeStruct((listed, 2, OBS, OBS), F32),
        ),
        in_specs=[VMEM, HBM],
        out_specs=(VMEM, HBM),
        scratch_shapes=[
            pltpu.VMEM((PAIRS, HALF, 128), F32),
            pltpu.VMEM((PAIRS, HALF, 128), F32),
            pltpu.VMEM((RING - 1, HALF, 128), F32),
            pltpu.VMEM((HALF, 128), F32),
            pltpu.VMEM((RING - 1, HALF, 128), F32),
            DMA, DMA,
            DMA((RING - 1,)), DMA((RING - 1,)),
            DMA((RING - 1,)), DMA((RING - 1,)),
            DMA((RING - 1,)), DMA((RING - 1,)),
            DMA((BANDS - 1, PAIRS)), DMA((BANDS - 1, PAIRS)),
            DMA((BANDS, PAIRS)), DMA((BANDS, PAIRS)),
            DMA((BANDS - 1,)), DMA((BANDS - 1,)),
            DMA((BANDS - 1,)), DMA((BANDS - 1,)),
        ],
        compiler_params=pltpu.CompilerParams(collective_id=collective_id, has_side_effects=True),
    )(packet, rows)


def local(anomalies, state_mean, obs_value, obs_cell, owner, order, root_inv, gain_inv):
    flat = anomalies.reshape(MEMBERS * GROUPS, 128)
    mean = state_mean.reshape(GROUPS, 128)
    values = jnp.concatenate([obs_value, obs_value], axis=1)
    packet, rows, table = pl.pallas_call(
        prep_kernel,
        name="prep",
        out_shape=(
            jax.ShapeDtypeStruct((PAIRS, ROWS, 128), F32),
            jax.ShapeDtypeStruct((BATCHES, 2, QUARTER, OBS), F32),
            jax.ShapeDtypeStruct((32,), jnp.int32),
        ),
        in_specs=[SMEM, SMEM, VMEM, VMEM, VMEM, VMEM, HBM, HBM],
        out_specs=(VMEM, HBM, SMEM),
        scratch_shapes=[
            pltpu.VMEM((ROWS, CELLS), F32),
            pltpu.VMEM((BATCHES, 2, QUARTER, OBS), F32),
            pltpu.SMEM((BATCHES,), jnp.int32),
            DMA((BATCHES, 2)),
            DMA((BATCHES,)),
        ],
    )(order, owner, flat, mean, obs_cell, values, root_inv, gain_inv)
    spread, full = exchange(BATCHES, 1, packet, rows)
    out_flat, out_mean = pl.pallas_call(
        solve_kernel,
        name="solve",
        out_shape=(
            jax.ShapeDtypeStruct((MEMBERS * GROUPS, 128), F32),
            jax.ShapeDtypeStruct((GROUPS, 128), F32),
        ),
        in_specs=[SMEM, SMEM, VMEM, VMEM, VMEM, VMEM, HBM, HBM],
        out_specs=(VMEM, VMEM),
        scratch_shapes=[
            pltpu.VMEM((ROWS, CELLS), F32),
            pltpu.VMEM((BATCHES, ROWS, OBS), F32),
            pltpu.VMEM((BATCHES, 2, OBS, OBS), F32),
            pltpu.VMEM((GROUPS * ROWS, OBS), BF16),
            pltpu.VMEM((GROUPS * ROWS, OBS), BF16),
            pltpu.VMEM((GROUPS * ROWS, ROWS), F32),
            DMA((BATCHES, BANDS)),
        ],
    )(owner, table, flat, mean, obs_cell, spread, rows, full)
    return out_flat.reshape(anomalies.shape), out_mean.reshape(state_mean.shape)


def solution(mesh):
    return jax.shard_map(
        local,
        mesh=mesh,
        in_specs=(
            P(None, "gx", "gy", None),
            P("gx", "gy", None),
            P(None, "gy"),
            P(),
            P(),
            P(),
            P(None, "gy", None),
            P(None, "gy", None),
        ),
        out_specs=(P(None, "gx", "gy", None), P("gx", "gy", None)),
        check_vma=False,
    )
```

time: 1050 us -> 96.1 us (0.09); the launches traced: 1040 us -> 95.8 us
  starting transfers between devices: 526 us -> 0 us
  blocking collectives: 292 us -> 0 us
  local copies, waits for them, and re-layouts: 98.2 us -> 0 us
  Pallas kernels: 0 us -> 93.7 us
  loops' own time: 62 us -> 0 us
  matrix products: 51.1 us -> 0 us
    ppermute x96 -> x0, starting transfers between devices: 526 us -> none  [shifted(): return lax.ppermute(value, axis, pairs)]
    all_gather x32 -> x0, blocking collectives: 292 us -> none  [gather_turned(): out, at, done = (lax.all_gather(both, axis, axis=0, tiled=True), 0, [])]
    pallas_call x0 -> x3, Pallas kernels: none -> 93.7 us  [the longest x1 76.6 us: exchange(): pl.pallas_call(functools.partial(comm_kernel, listed), name='exchange', o...]
    another operation x17 -> x0, loops' own time: 62 us -> none  [the longest x1 58.9 us: local(): lax.fori_loop(0, BATCHES, assimilate, (start_rows, start_mean))]
    dynamic_slice x96 -> x0, local copies, waits for them, and re-layouts: 60.4 us -> none  [the longest x16 21 us: assimilate(): root_slab = owner[batch_id]]
    dot_general x40 -> x0, matrix products: 51.1 us -> none  [product(): jnp.dot(left_side, right_side, precision=lax.Precision.HIGHEST, preferred...]
    gather x48 -> x0, local copies, waits for them, and re-layouts: 23.6 us -> none  [the longest x32 14 us: assimilate(): innovation = obs_value[batch_id] - jnp.take(mean_row, local_ids)]
  transfers between devices with their start and end apart: 96 -> 0, of which waited for: 0 -> 0; matrix products, arithmetic and copies ran while one was open for 0% -> 0% of each run, Pallas kernels for 0% -> 0%
where the time goes in v1:
time: 96.1 us; the launch traced here: 95.8 us
  Pallas kernels  93.7 us (98%)
  other arithmetic  1.45 us (2%)
    pallas_call x1, Pallas kernels, exchange(): pl.pallas_call(functools.partial(comm_kernel, listed), name='exchange', o...  76.6 us
    pallas_call x1, Pallas kernels, local(): pl.pallas_call(solve_kernel, name='solve', out_shape=(jax.ShapeDtypeStruc...  10.7 us
    pallas_call x1, Pallas kernels, local(): pl.pallas_call(prep_kernel, name='prep', out_shape=(jax.ShapeDtypeStruct(...  6.44 us

profile of v1, /device:TPU:1, one launch (start us, length us, event | category | flops | bytes accessed | tf_op | source)
XLA Modules:
  0.0 95.8 jit_solution(17707523164944716427)
XLA Ops:
  0.6 1.4 %pad_maximum_fusion.value_ref = f32[16,128]{1,0:T(8,128)} fusion(f32[16,64]{1,0:T(8,128)} %param.10), kind=kLoop, calls=%fused_computation | loop fusion | flops 2048 | bytes 12288 | tf_op jit(solution)/shard_map/concatenate | solution.py:439
  2.1 6.4 %prep.1 = (f32[8,96,128]{2,1,0:T(8,128)}, f32[16,2,64,256]{3,2,1,0:T(8,128)}, s32[32]{0:T(128)}) custom-call(s32[16]{0:T(128)} %order_s.1, s32[16]{0:T(128)} %owner_s.3, f32[1280,128]{1,0:T(8,128)} %bitcast.4, f32[16,128]{1,0:T(8,128)} %bitcast.6, s32[16,256]{1,0:T(8,128)} %cell_ref.3, f32[16,128]{1,0:T(8,128)} %pad_maximum_fusion.value_ref, ...), custom_call_target="tpu_custom_call" | custom-call | tf_op jit(solution)/shard_map/prep/pallas_call | solution.py:440
  8.5 76.6 %exchange.1 = (f32[4,8,96,128]{3,2,1,0:T(8,128)}, f32[16,2,256,256]{3,2,1,0:T(8,128)}) custom-call(f32[8,96,128]{2,1,0:T(8,128)} %get-tuple-element.10.packet_ref, f32[16,2,64,256]{3,2,1,0:T(8,128)} %get-tuple-element.11.rows_ref), custom_call_target="tpu_custom_call" | custom-call | tf_op jit(solution)/shard_map/exchange/pallas_call | solution.py:408
  85.1 10.7 %solve.1 = (f32[1280,128]{1,0:T(8,128)}, f32[16,128]{1,0:T(8,128)}) custom-call(s32[16]{0:T(128)} %owner_s.3, s32[32]{0:T(128)} %get-tuple-element.9.table_s, f32[1280,128]{1,0:T(8,128)} %bitcast.5, f32[16,128]{1,0:T(8,128)} %bitcast.7, s32[16,256]{1,0:T(8,128)} %cell_ref.3, f32[4,8,96,128]{3,2,1,0:T(8,128)} %get-tuple-element.12.spread_ref, ...), custom_call_target="tpu_custom_call" | custom-call | tf_op jit(solution)/shard_map/solve/pallas_call | solution.py:459
